TPU v7x, 1024 devices: a whole 4x8x16 slice. The times are simulated.
1024 devices in a mesh: group: 32 (over x, y_hi, core), resp: 32 (over z, y_lo).
Axes of the slice: x: 4, y: 8 (y_hi: 4, y_lo: 2; y = y_hi * 2 + y_lo), z: 16, core: 2. Of those that a mesh axis runs over, the one named last changes fastest.
Arguments:
- prompt_hidden: bfloat16 [32, 256, 4096], P('group', 'resp'), may hold values from -6 to 6
- kv_weight: bfloat16 [2048, 4096], P('resp'), may hold values from -0.09375 to 0.09375
- queries: bfloat16 [32, 4096, 4096], P('group', 'resp'), may hold values from -150 to 150
- resp_keys: bfloat16 [32, 4096, 1024], P('group', 'resp'), may hold values from -5 to 5
- resp_values: bfloat16 [32, 4096, 1024], P('group', 'resp'), may hold values from -6 to 6
- upstream: bfloat16 [32, 4096, 4096], P('group', 'resp'), may hold values from -6 to 6
- signs: int32 [32, 4096], P('group', 'resp'), may hold values from -1 to 1
- lengths: int32 [32, 32], P('group', 'resp'), may hold values from 64 to 128
Outputs:
- grad_keys: bfloat16 [32, 4096, 1024], P('group', 'resp')
- grad_values: bfloat16 [32, 4096, 1024], P('group', 'resp')
- grad_weight: float32 [2048, 4096], P('resp', 'group')
All inputs are finite; a program needn't handle non-finite values.
Results may differ from a plain program's by a relative error of at most 0.025.
Values may be sent and summed in bfloat16 or wider, within the bound.
A program may use at most 32 MiB of HBM per device.

v0:
```python
import math

import jax
import jax.numpy as jnp
from jax import lax
from jax.sharding import Mesh
from jax.sharding import PartitionSpec as P

HEADS = 32
KV_HEADS = 8
HEAD = 128
RESP = ("resp_0", "resp_1")


def gathered_by_axis(value, axes, dim):
    for axis in reversed(axes):
        value = lax.all_gather(value, axis, axis=dim, tiled=True)
    return value


def summed_rows(value, axes, dim):
    for axis in axes:
        value = lax.psum_scatter(value, axis, scatter_dimension=dim, tiled=True)
    return value


def cut_along(value, dim, length):
    before, after = (value.shape[:dim], value.shape[dim + 1 :])
    return jnp.moveaxis(value.reshape(*before, length, -1, *after), dim, 0)


def sent_and_summed(value, axis, dim):
    blocks = cut_along(value, dim, lax.axis_size(axis))
    arrived = lax.all_to_all(blocks, axis, split_axis=0, concat_axis=0, tiled=True)
    return arrived.sum(axis=0)


def attend_group(inputs):
    queries, cotangent, own_keys, own_values, prompt_keys, prompt_values = inputs
    seq_len = queries.shape[0]
    scaling = 1.0 / math.sqrt(queries.shape[-1])
    prompt_scores = (
        jnp.einsum("rqd,dp->qrp", queries, prompt_keys, preferred_element_type=jnp.float32)
        * scaling
    )
    own_scores = (
        jnp.einsum("rqd,sd->qrs", queries, own_keys, preferred_element_type=jnp.float32) * scaling
    )
    causal = lax.broadcasted_iota(jnp.int32, (seq_len, seq_len), 0) >= lax.broadcasted_iota(
        jnp.int32, (seq_len, seq_len), 1
    )
    own_scores = jnp.where(causal, own_scores, -jnp.inf)
    highest = jnp.maximum(jnp.max(prompt_scores, axis=-1), jnp.max(own_scores, axis=-1))[..., None]
    prompt_exp = jnp.exp(prompt_scores - highest)
    own_exp = jnp.exp(own_scores - highest)
    denominator = (jnp.sum(prompt_exp, axis=-1) + jnp.sum(own_exp, axis=-1))[..., None]
    prompt_probs = prompt_exp / denominator
    own_probs = own_exp / denominator
    prompt_half = prompt_probs.astype(jnp.bfloat16)
    own_half = own_probs.astype(jnp.bfloat16)
    mixed = jnp.einsum(
        "qrp,dp->qrd", prompt_half, prompt_values, preferred_element_type=jnp.float32
    )
    mixed = mixed + jnp.einsum(
        "qrs,sd->qrd", own_half, own_values, preferred_element_type=jnp.float32
    )
    delta = jnp.einsum("qrd,rqd->qr", mixed, cotangent.astype(jnp.float32))[..., None]
    prompt_dots = jnp.einsum(
        "rqd,dp->qrp", cotangent, prompt_values, preferred_element_type=jnp.float32
    )
    own_dots = jnp.einsum("rqd,sd->qrs", cotangent, own_values, preferred_element_type=jnp.float32)
    prompt_sgrad = (prompt_probs * (prompt_dots - delta)).astype(jnp.bfloat16)
    own_sgrad = (own_probs * (own_dots - delta)).astype(jnp.bfloat16)
    key_terms = (
        jnp.einsum("qrp,rqd->dp", prompt_sgrad, queries, preferred_element_type=jnp.float32)
        * scaling
    )
    value_terms = jnp.einsum(
        "qrp,rqd->dp", prompt_half, cotangent, preferred_element_type=jnp.float32
    )
    key_grads = (
        jnp.einsum("qrs,rqd->sd", own_sgrad, queries, preferred_element_type=jnp.float32) * scaling
    ).astype(jnp.bfloat16)
    value_grads = jnp.einsum(
        "qrs,rqd->sd", own_half, cotangent, preferred_element_type=jnp.float32
    ).astype(jnp.bfloat16)
    return (key_terms, value_terms, key_grads, value_grads)


def per_device(prompt_hidden, kv_weight, queries, resp_keys, resp_values, upstream, signs, lengths):
    own_rows = prompt_hidden[0]
    kept_rows = gathered_by_axis(own_rows, RESP, 0)
    projected = lax.dot_general(
        kv_weight, kept_rows, (((1,), (1,)), ((), ())), preferred_element_type=jnp.float32
    )
    prompt_kv = gathered_by_axis(projected.astype(jnp.bfloat16), RESP, 0)
    key_width = KV_HEADS * HEAD
    per_head = HEADS // KV_HEADS
    seq_len = queries.shape[1]
    prompt_keys = prompt_kv[:key_width].reshape(KV_HEADS, HEAD, -1)
    prompt_values = prompt_kv[key_width:].reshape(KV_HEADS, HEAD, -1)
    live_rows = (lax.broadcasted_iota(jnp.int32, (seq_len,), 0) < lengths[0, 0]).astype(jnp.int32)
    weights = (signs[0] * live_rows).astype(jnp.bfloat16)
    cotangent = upstream[0] * weights[:, None]
    query_heads = jnp.moveaxis(queries[0].reshape(seq_len, KV_HEADS, per_head, HEAD), 1, 0)
    cotangent_heads = jnp.moveaxis(cotangent.reshape(seq_len, KV_HEADS, per_head, HEAD), 1, 0)
    own_keys = jnp.moveaxis(resp_keys[0].reshape(seq_len, KV_HEADS, HEAD), 1, 0)
    own_values = jnp.moveaxis(resp_values[0].reshape(seq_len, KV_HEADS, HEAD), 1, 0)
    key_terms, value_terms, key_grads, value_grads = lax.map(
        attend_group,
        (query_heads, cotangent_heads, own_keys, own_values, prompt_keys, prompt_values),
    )
    prompt_terms = jnp.concatenate(
        [key_terms.reshape(key_width, -1), value_terms.reshape(key_width, -1)], axis=0
    )
    prompt_grad = summed_rows(prompt_terms, RESP, 0).astype(jnp.bfloat16)
    weight_terms = jnp.dot(prompt_grad, kept_rows, preferred_element_type=jnp.float32)
    grad_weight = sent_and_summed(weight_terms, "group", 1)
    grad_keys = jnp.moveaxis(key_grads, 0, 1).reshape(1, seq_len, key_width)
    grad_values = jnp.moveaxis(value_grads, 0, 1).reshape(1, seq_len, key_width)
    return (grad_keys, grad_values, grad_weight)


def solution(mesh):
    torus = Mesh(mesh.devices.reshape(mesh.shape["group"], 16, 2), ("group", "resp_0", "resp_1"))
    return jax.shard_map(
        per_device,
        mesh=torus,
        in_specs=(
            P("group", RESP, None),
            P(RESP, None),
            P("group", RESP, None),
            P("group", RESP, None),
            P("group", RESP, None),
            P("group", RESP, None),
            P("group", RESP),
            P("group", RESP),
        ),
        out_specs=(P("group", RESP, None), P("group", RESP, None), P(RESP, "group")),
        check_vma=False,
    )
```

profile of v0, /device:TPU:8, one launch (start us, length us, event | category | flops | bytes accessed | tf_op | source)
XLA Modules:
  0.0 418.5 jit_solution(872877629263350647)
XLA Ops:
  7.3 17.9 %all-gather = bf16[1,16,4096]{2,1,0:T(8,128)(2,1)} all-gather(bf16[1,8,4096]{2,1,0:T(8,128)(2,1)} %param.10), channel_id=2, replica_groups=mesh['group'=32,'resp_0'=16,'resp_1'=2] {'resp_1'}, dimensions={1}, use_global_device_ids=true | all-gather | bytes 196608 | tf_op jit(solution)/shard_map/all_gather | solution.py:17
  25.2 72.1 %all-gather.7.cloned.1.call-done = bf16[1,256,4096]{2,1,0:T(8,128)(2,1)} async-done(((bf16[1,16,4096]{2,1,0:T(8,128)(2,1)}), bf16[1,256,4096]{2,1,0:T(8,128)(2,1)}) %all-gather.7.cloned.1.call-update) | async-done | bytes 2097168 | tf_op jit(solution)/shard_map/all_gather | solution.py:17
  97.3 2.3 fusion.84
  99.7 4.7 %all_gather.14 = bf16[128,256]{1,0:T(8,128)(2,1)} all-gather(bf16[64,256]{1,0:T(8,128)(2,1)S(1)} %fusion.84), channel_id=1, replica_groups=mesh['group'=32,'resp_0'=16,'resp_1'=2] {'resp_1'}, dimensions={0}, use_global_device_ids=true | all-gather | bytes 98304 | tf_op jit(solution)/shard_map/all_gather | solution.py:17
  109.6 65.6 %all-gather.5.cloned.1.call-done = bf16[2048,256]{1,0:T(8,128)(2,1)} async-done(((bf16[128,256]{1,0:T(8,128)(2,1)}), bf16[2048,256]{1,0:T(8,128)(2,1)}) %all-gather.5.cloned.1.call-update) | async-done | bytes 1048592 | tf_op jit(solution)/shard_map/all_gather | solution.py:17
  175.2 2.1 fusion.91
  177.2 91.7 %while.16 = (s32[]{:T(128)}, f32[8,128,256]{2,1,0:T(8,128)}, f32[8,128,256]{2,1,0:T(8,128)}, bf16[8,128,128]{2,1,0:T(8,128)(2,1)}, bf16[8,128,128]{2,1,0:T(8,128...) while((s32[]{:T(128)}, f32[8,128,256]{2,1,0:T(8,128)}, ...), condition=%wide.region_5.6_spmd, body=%wide.region_0.5_spmd.sunk | while | flops 254638592 | bytes 7137417 | solution.py:109
  181.3 1.9 fusion.143
  184.9 2.0 fusion.141
  192.8 1.9 fusion.143
  196.4 2.0 fusion.141
  204.2 1.9 fusion.143
  207.8 2.0 fusion.141
  219.3 2.0 fusion.141
  230.8 2.0 fusion.141
  238.7 1.9 fusion.143
  242.3 2.0 fusion.141
  253.7 2.0 fusion.141
  265.2 2.0 fusion.141
  269.0 3.0 pad_maximum_fusion
  272.0 74.6 %reduce-scatter.3.cloned.1.call-done = f32[128,256]{1,0:T(8,128)} async-done(((f32[2048,256]{1,0:T(8,128)}), f32[128,256]{1,0:T(8,128)}) %reduce-scatter.3.cloned.1.call-update) | async-done | bytes 131088 | tf_op jit(solution)/shard_map/reduce_scatter | solution.py:23
  346.7 24.8 %reduce-scatter.5.cloned.1.call-done = f32[64,256]{1,0:T(8,128)} async-done(((f32[128,256]{1,0:T(8,128)}), f32[64,256]{1,0:T(8,128)}) %reduce-scatter.5.cloned.1.call-update) | async-done | bytes 65552 | tf_op jit(solution)/shard_map/reduce_scatter | solution.py:23
  374.0 7.4 %all-to-all-start = ((f32[32,64,128]{2,1,0:T(8,128)}), f32[32,64,128]{2,1,0:T(8,128)S(1)}, u32[]{:S(2)}, u32[]{:S(2)}) async-start(f32[32,64,128]{2,1,0:T(8,128)} %bitcast.196), calls=%async_computation.2 | async-start | bytes 2097152 | tf_op jit(solution)/shard_map/all_to_all | solution.py:34
  383.5 27.9 %all-to-all-done = f32[32,64,128]{2,1,0:T(8,128)S(1)} async-done(((f32[32,64,128]{2,1,0:T(8,128)}), f32[32,64,128]{2,1,0:T(8,128)S(1)}, u32[]{:S(2)}, u32[]{:S(2)}) %all-to-all-start) | async-done | bytes 1048608 | tf_op jit(solution)/shard_map/all_to_all | solution.py:34
  (157 shorter events, 77.7 us)
Async XLA Ops:
  7.2 90.2 %copy-start = (bf16[64,4096]{1,0:T(8,128)(2,1)S(1)}, bf16[64,4096]{1,0:T(8,128)(2,1)}, u32[]{:S(2)}) copy-start(bf16[64,4096]{1,0:T(8,128)(2,1)} %param.11) | copy-start | bytes 1572868
  7.2 98.0 %copy-start.3 = (bf16[1,128,1024]{2,1,0:T(8,128)(2,1)S(1)}, bf16[1,128,1024]{2,1,0:T(8,128)(2,1)}, u32[]{:S(2)}) copy-start(bf16[1,128,1024]{2,1,0:T(8,128)(2,1)} %param.13) | copy-start | bytes 786436
  7.2 98.1 %copy-start.4 = (bf16[1,128,1024]{2,1,0:T(8,128)(2,1)S(1)}, bf16[1,128,1024]{2,1,0:T(8,128)(2,1)}, u32[]{:S(2)}) copy-start(bf16[1,128,1024]{2,1,0:T(8,128)(2,1)} %param.14) | copy-start | bytes 786436
  7.2 99.0 %copy-start.2 = (bf16[1,128,4096]{2,1,0:T(8,128)(2,1)S(1)}, bf16[1,128,4096]{2,1,0:T(8,128)(2,1)}, u32[]{:S(2)}) copy-start(bf16[1,128,4096]{2,1,0:T(8,128)(2,1)} %param.12) | copy-start | bytes 3145732
  7.2 90.1 %all-gather.7.cloned.1.call-start = ((), (), s32[]{:S(2)}) async-start(), calls=%async_computation.6 | async-start | bytes 2228224 | tf_op jit(solution)/shard_map/all_gather | solution.py:17
  25.2 150.0 %all-gather.5.cloned.1.call-start = ((), (), s32[]{:S(2)}) async-start(), calls=%async_computation.3 | async-start | bytes 1114112 | tf_op jit(solution)/shard_map/all_gather | solution.py:17
  104.4 242.3 %reduce-scatter.3.cloned.1.call-start = ((), (), s32[]{:S(2)}) async-start(), calls=%async_computation.4 | async-start | bytes 2228224 | tf_op jit(solution)/shard_map/reduce_scatter | solution.py:23
  106.2 2.3 copy-start.7
  272.0 99.6 %copy-start.1 = (bf16[1,256,4096]{2,1,0:T(8,128)(2,1)S(1)}, bf16[1,256,4096]{2,1,0:T(8,128)(2,1)}, u32[]{:S(2)}) copy-start(bf16[1,256,4096]{2,1,0:T(8,128)(2,1)} %all-gather.7.cloned.1.call-done) | copy-start | bytes 6291460
  272.0 99.6 %reduce-scatter.5.cloned.1.call-start = ((), (), s32[]{:S(2)}) async-start(), calls=%async_computation.5 | async-start | bytes 196608 | tf_op jit(solution)/shard_map/reduce_scatter | solution.py:23
  372.9 8.6 %copy-start.5 = (bf16[8,128,128]{2,1,0:T(8,128)(2,1)S(1)}, bf16[8,128,128]{2,1,0:T(8,128)(2,1)}, u32[]{:S(2)}) copy-start(bf16[8,128,128]{2,1,0:T(8,128)(2,1)} %get-tuple-element.64) | copy-start | bytes 786436
  374.0 8.5 %copy-start.6 = (bf16[8,128,128]{2,1,0:T(8,128)(2,1)S(1)}, bf16[8,128,128]{2,1,0:T(8,128)(2,1)}, u32[]{:S(2)}) copy-start(bf16[8,128,128]{2,1,0:T(8,128)(2,1)} %get-tuple-element.63) | copy-start | bytes 786436
  374.0 37.3 %all-to-all-start = ((f32[32,64,128]{2,1,0:T(8,128)}), f32[32,64,128]{2,1,0:T(8,128)S(1)}, u32[]{:S(2)}, u32[]{:S(2)}) async-start(f32[32,64,128]{2,1,0:T(8,128)} %bitcast.196), calls=%async_computation.2 | async-start | bytes 2097152 | tf_op jit(solution)/shard_map/all_to_all | solution.py:34
Sparse Core Ops, SparseCore 0:
  25.3 72.0 all-gather.6
  104.5 70.6 all-gather.4
  272.1 74.5 reduce-scatter.2
  349.9 21.6 reduce-scatter.4
where the time goes:
time: 421 us; the launch traced here: 419 us
  waiting for transfers between devices  265 us (63%)
  matrix products  84.4 us (20%)
  blocking collectives  22.6 us (5%)
  local copies, waits for them, and re-layouts  16.9 us (4%)
  between operations  14.6 us (3%)
  starting transfers between devices  7.61 us (2%)
  other arithmetic  6.95 us (2%)
    all_gather x2, waiting for transfers between devices, gathered_by_axis(): value = lax.all_gather(value, axis, axis=dim, tiled=True)  138 us
    reduce_scatter x2, waiting for transfers between devices, summed_rows(): value = lax.psum_scatter(value, axis, scatter_dimension=dim, tiled=True)  99.5 us
    all_to_all x1, waiting for transfers between devices, sent_and_summed(): lax.all_to_all(blocks, axis, split_axis=0, concat_axis=0, tiled=True)  27.9 us
    all_gather x2, blocking collectives, gathered_by_axis(): value = lax.all_gather(value, axis, axis=dim, tiled=True)  22.6 us
    dot_general x8, matrix products, attend_group(): jnp.einsum('qrp,rqd->dp', prompt_sgrad, queries, preferred_element_type=j...  15.8 us
    dot_general x8, matrix products, attend_group(): jnp.einsum('qrs,rqd->sd', own_sgrad, queries, preferred_element_type=jnp....  15.2 us
    dot_general x8, matrix products, attend_group(): jnp.einsum('qrp,rqd->dp', prompt_half, cotangent, preferred_element_type=...  14.3 us
    dot_general x8, matrix products, attend_group(): jnp.einsum('qrs,rqd->sd', own_half, cotangent, preferred_element_type=jnp...  13.7 us
  transfers between devices with their start and end apart: 5, of which 5 were waited for; matrix products, arithmetic and copies ran while one was open for 2% of the time, Pallas kernels for 0%

commit v1 on v0

v1 whole, which is shorter than its diff:
```python
import functools
import math

import jax
import jax.numpy as jnp
from jax import lax
from jax.experimental import pallas as pl
from jax.experimental.pallas import tpu as pltpu
from jax.sharding import PartitionSpec as P

MESH = pl.DeviceIdType.MESH
F32 = jnp.float32
BF16 = jnp.bfloat16
KV_HEADS = 8
PER_HEAD = 4
HEAD = 128
D = 4096
SEQ = 128
PROMPT = 256
NZ = 16
NCHIP = 16
NCH = 4
NOTHER = 2
CW = D // NCH
RIGHT, LEFT = 0, 1


def kernel(
    hid_in, w_in, q_in, rk_in, rv_in, up_in, signs_in, len_in,
    gk_out, gv_out, gw_out,
    hid, hid2, wbuf, q, rk, rv, cot, qt, ct, kt_own, vt_own,
    kvb, ph, ds, terms, yrecv, esend, erecv, own32, dsend, drecv, gsend, grecv,
    load_sem, a_send, a_recv, ay_send, ay_recv, c_send, c_recv, cy_send, cy_recv,
    e_send, e_recv, ey_send, ey_recv, d_send, d_recv, g_send, g_recv,
):
    g = lax.axis_index("group")
    r = lax.axis_index("resp")
    z, y = r // 2, lax.rem(r, 2)
    chip, core = g // 2, lax.rem(g, 2)

    def zmod(value):
        return lax.rem(value + 2 * NZ, NZ)

    up_z = {"resp": zmod(z + 1) * 2 + y}
    down_z = {"resp": zmod(z - 1) * 2 + y}
    partner = {"resp": z * 2 + 1 - y}
    twin = {"group": chip * 2 + 1 - core}
    to = (up_z, down_z)
    sign = (-1, 1)

    def peer(i):
        return lax.rem(chip + i, NCHIP)

    loads = [
        pltpu.make_async_copy(hid_in, hid.at[y, z], load_sem.at[0]),
        pltpu.make_async_copy(w_in, wbuf, load_sem.at[1]),
        pltpu.make_async_copy(q_in, q, load_sem.at[2]),
        pltpu.make_async_copy(up_in, cot, load_sem.at[3]),
        pltpu.make_async_copy(rk_in, rk, load_sem.at[4]),
        pltpu.make_async_copy(rv_in, rv, load_sem.at[5]),
    ]
    for load in loads:
        load.start()

    barrier = pltpu.get_barrier_semaphore()
    for target in (up_z, down_z, partner, twin):
        pl.semaphore_signal(barrier, inc=1, device_id=target, device_id_type=MESH)

    def greet(i, carry):
        pl.semaphore_signal(
            barrier, inc=1, device_id={"group": peer(i) * 2 + core}, device_id_type=MESH
        )
        return carry

    lax.fori_loop(1, NCHIP, greet, 0)
    pl.semaphore_wait(barrier, NCHIP - 1 + 4)
    loads[0].wait()

    def hid_piece(col, zz, c):
        return hid.at[col, zz, :, pl.ds(c * CW, CW)]

    def a_copy(d, s, slot, col, zz, c):
        return pltpu.make_async_remote_copy(
            src_ref=hid_piece(col, zz, c), dst_ref=hid_piece(col, zz, c),
            send_sem=a_send.at[d, s, slot], recv_sem=a_recv.at[d, s, slot],
            device_id=to[d], device_id_type=MESH,
        )

    def ay_copy(col, zz, c):
        return pltpu.make_async_remote_copy(
            src_ref=hid_piece(col, zz, c), dst_ref=hid_piece(col, zz, c),
            send_sem=ay_send.at[zz, c], recv_sem=ay_recv.at[zz, c],
            device_id=partner, device_id_type=MESH,
        )

    slots = [(0, c) for c in range(NCH)] + [(1, c) for c in range(NOTHER)]

    def column(kind):
        return y if kind == 0 else 1 - y

    def carried(d, slot, s_last):
        kind, c = slots[slot]
        if not s_last:
            return True
        half = (NCH if kind == 0 else NOTHER) // 2
        return (c < half) == (d == RIGHT)

    for c in range(NCH):
        ay_copy(y, z, c).start()
    for slot, (kind, c) in enumerate(slots):
        for d in (RIGHT, LEFT):
            if kind == 1 and d == RIGHT:
                ay_copy(1 - y, z, c).wait_recv()
            a_copy(d, 0, slot, column(kind), z, c).start()

    def a_step(s, last):
        for slot, (kind, c) in enumerate(slots):
            for d in (RIGHT, LEFT):
                zz = zmod(z + sign[d] * s)
                a_copy(d, s - 1, slot, column(kind), zz, c).wait_recv()
                if carried(d, slot, last):
                    a_copy(d, s, slot, column(kind), zz, c).start()
                if kind == 0 and c >= NOTHER:
                    ay_copy(y, zz, c).start()

    def prepare(j):
        weights = jnp.where(
            lax.broadcasted_iota(jnp.int32, (1, SEQ), 1) < len_in[...], signs_in[...], 0
        ).astype(F32)
        weights = jnp.broadcast_to(weights, (SEQ, SEQ)).T.astype(BF16)
        for i in range(PER_HEAD):
            cols = pl.ds(pl.multiple_of((j * PER_HEAD + i) * HEAD, HEAD), HEAD)
            qt[j, :, i * SEQ:(i + 1) * SEQ] = q[:, cols].T
            value = cot[:, cols] * weights
            cot[:, cols] = value
            ct[j, :, i * SEQ:(i + 1) * SEQ] = value.T
        cols = pl.ds(pl.multiple_of(j * HEAD, HEAD), HEAD)
        kt_own[j] = rk[:, cols].T
        vt_own[j] = rv[:, cols].T

    for load in loads[1:]:
        load.wait()
    prepare(0)

    def a_loop(s, carry):
        a_step(s, False)
        prepare(s)
        return carry

    lax.fori_loop(1, 7, a_loop, 0)
    a_step(7, True)
    prepare(7)
    far = zmod(z + 8)
    for slot, (kind, c) in enumerate(slots):
        d = RIGHT if carried(RIGHT, slot, True) else LEFT
        a_copy(d, 7, slot, column(kind), far, c).wait_recv()
        if kind == 0 and c >= NOTHER:
            ay_copy(y, far, c).start()
    for c in range(NOTHER, NCH):
        ay_copy(1 - y, z, c).wait_recv()

    def ay_wait(i, carry):
        for c in range(NOTHER, NCH):
            ay_copy(1 - y, zmod(z + i), c).wait_recv()
        return carry

    lax.fori_loop(1, NZ, ay_wait, 0)

    kw = 512
    total = jnp.zeros((64, PROMPT), F32)

    def project(i, total):
        cols = pl.ds(pl.multiple_of(i * kw, kw), kw)
        rows = hid[:, :, :, cols].astype(F32).reshape(PROMPT, kw).astype(BF16)
        hid2[:, cols] = rows
        return total + lax.dot_general(
            wbuf[:, cols], rows, (((1,), (1,)), ((), ())), preferred_element_type=F32
        )

    total = lax.fori_loop(0, D // kw, project, total)
    kvb[z, y] = total.astype(BF16)

    def kv_piece(zz, col, c):
        return kvb.at[zz, col, pl.ds(c * 32, 32), :]

    def c_copy(d, s, c, zz):
        return pltpu.make_async_remote_copy(
            src_ref=kv_piece(zz, y, c), dst_ref=kv_piece(zz, y, c),
            send_sem=c_send.at[d, s, c], recv_sem=c_recv.at[d, s, c],
            device_id=to[d], device_id_type=MESH,
        )

    def cy_copy(zz, col, c):
        return pltpu.make_async_remote_copy(
            src_ref=kv_piece(zz, col, c), dst_ref=kv_piece(zz, col, c),
            send_sem=cy_send.at[zz, c], recv_sem=cy_recv.at[zz, c],
            device_id=partner, device_id_type=MESH,
        )

    for c in range(2):
        for d in (RIGHT, LEFT):
            c_copy(d, 0, c, z).start()
        cy_copy(z, y, c).start()

    def c_step(s, last):
        for c in range(2):
            for d in (RIGHT, LEFT):
                zz = zmod(z + sign[d] * s)
                c_copy(d, s - 1, c, zz).wait_recv()
                if not last or c == d:
                    c_copy(d, s, c, zz).start()
                cy_copy(zz, y, c).start()

    def c_loop(s, carry):
        c_step(s, False)
        return carry

    lax.fori_loop(1, 7, c_loop, 0)
    c_step(7, True)
    for c in range(2):
        c_copy(c, 7, c, far).wait_recv()
        cy_copy(far, y, c).start()

    def cy_wait(i, carry):
        for c in range(2):
            cy_copy(zmod(z + i), 1 - y, c).wait_recv()
        return carry

    lax.fori_loop(0, NZ, cy_wait, 0)

    scaling = 1.0 / math.sqrt(HEAD)
    factor = scaling * math.log2(math.e)

    def attend(j, carry):
        keys = jnp.concatenate([kvb[j].reshape(HEAD, PROMPT), kt_own[j]], axis=1)
        values = jnp.concatenate([kvb[j + 8].reshape(HEAD, PROMPT), vt_own[j]], axis=1)
        shape = (SEQ, PROMPT + SEQ)
        at = lax.broadcasted_iota(jnp.int32, shape, 0)
        key_at = lax.broadcasted_iota(jnp.int32, shape, 1) - PROMPT
        seen = key_at <= at
        for i in range(PER_HEAD):
            cols = pl.ds(pl.multiple_of((j * PER_HEAD + i) * HEAD, HEAD), HEAD)
            rows = slice(i * SEQ, (i + 1) * SEQ)
            scores = jnp.dot(q[:, cols], keys, preferred_element_type=F32)
            scores = jnp.where(seen, scores, -jnp.inf)
            highest = jnp.max(scores, axis=1, keepdims=True)
            weight = jnp.exp2((scores - highest) * factor)
            probs = weight * (1.0 / jnp.sum(weight, axis=1, keepdims=True))
            half = probs.astype(BF16)
            ph[rows, :] = half
            dots = jnp.dot(cot[:, cols], values, preferred_element_type=F32)
            delta = jnp.sum(half.astype(F32) * dots, axis=1, keepdims=True)
            ds[rows, :] = (probs * (dots - delta)).astype(BF16)
        key_grad = jnp.dot(qt[j], ds[...], preferred_element_type=F32) * scaling
        value_grad = jnp.dot(ct[j], ph[...], preferred_element_type=F32)
        terms[j] = key_grad[:, :PROMPT].astype(BF16).reshape(2, 64, PROMPT)
        terms[j + 8] = value_grad[:, :PROMPT].astype(BF16).reshape(2, 64, PROMPT)
        cols = pl.ds(pl.multiple_of(j * HEAD, HEAD), HEAD)
        gk_out[:, cols] = key_grad[:, PROMPT:].T.astype(BF16)
        gv_out[:, cols] = value_grad[:, PROMPT:].T.astype(BF16)
        return carry

    lax.fori_loop(0, KV_HEADS, attend, 0)

    def ey_copy(zz, col):
        return pltpu.make_async_remote_copy(
            src_ref=terms.at[zz, col], dst_ref=yrecv.at[zz],
            send_sem=ey_send.at[zz], recv_sem=ey_recv.at[zz],
            device_id=partner, device_id_type=MESH,
        )

    def e_copy(d, s, c):
        part = pl.ds(c * 32, 32)
        return pltpu.make_async_remote_copy(
            src_ref=esend.at[d, s, part, :], dst_ref=erecv.at[d, s, part, :],
            send_sem=e_send.at[d, s, c], recv_sem=e_recv.at[d, s, c],
            device_id=to[d], device_id_type=MESH,
        )

    ey_copy(far, 1 - y).start()

    def ey_start(i, carry):
        ey_copy(zmod(z + 8 - i), 1 - y).start()
        ey_copy(zmod(z + 8 + i), 1 - y).start()
        return carry

    lax.fori_loop(1, 8, ey_start, 0)
    ey_copy(z, 1 - y).start()

    def pair_sum(zz, c):
        part = pl.ds(c * 32, 32)
        return terms[zz, y, part, :].astype(F32) + yrecv[zz, part, :].astype(F32)

    ey_copy(far, y).wait_recv()
    for d in (RIGHT, LEFT):
        esend[d, 0, pl.ds(d * 32, 32), :] = pair_sum(far, d).astype(BF16)
        e_copy(d, 0, d).start()

    def e_step(s, first):
        for d in (RIGHT, LEFT):
            ey_copy(zmod(z + sign[d] * (s - 8)), y).wait_recv()
        for c in range(2):
            part = pl.ds(c * 32, 32)
            for d in (RIGHT, LEFT):
                value = pair_sum(zmod(z + sign[d] * (s - 8)), c)
                if not first or c == d:
                    e_copy(d, s - 1, c).wait_recv()
                    value = value + erecv[d, s - 1, part, :].astype(F32)
                esend[d, s, part, :] = value.astype(BF16)
                e_copy(d, s, c).start()

    e_step(1, True)

    def e_loop(s, carry):
        e_step(s, False)
        return carry

    lax.fori_loop(2, 8, e_loop, 0)
    ey_copy(z, y).wait_recv()
    halves = []
    for c in range(2):
        part = pl.ds(c * 32, 32)
        value = pair_sum(z, c)
        for d in (RIGHT, LEFT):
            e_copy(d, 7, c).wait_recv()
            value = value + erecv[d, 7, part, :].astype(F32)
        halves.append(value.astype(BF16))
    prompt_grad = jnp.concatenate(halves, axis=0)

    def d_copy(b):
        part = pl.ds(b * 4, 4)
        return pltpu.make_async_remote_copy(
            src_ref=dsend.at[part], dst_ref=drecv.at[part],
            send_sem=d_send.at[b], recv_sem=d_recv.at[b],
            device_id=twin, device_id_type=MESH,
        )

    def g_copy(i):
        return pltpu.make_async_remote_copy(
            src_ref=gsend.at[i], dst_ref=grecv.at[i],
            send_sem=g_send.at[i], recv_sem=g_recv.at[i],
            device_id={"group": peer(i) * 2 + core}, device_id_type=MESH,
        )

    def weigh(i, carry):
        k = peer(i)
        cols = pl.ds(pl.multiple_of(k * 256, 256), 256)
        block = jnp.dot(prompt_grad, hid2[:, cols], preferred_element_type=F32)
        low, high = block[:, :128], block[:, 128:]
        own32[i] = jnp.where(core == 0, low, high)
        dsend[i] = jnp.where(core == 0, high, low).astype(BF16)
        return carry

    for b in range(4):
        lax.fori_loop(4 * b, 4 * b + 4, weigh, 0)
        d_copy(b).start()

    def send_out(i, carry):
        gsend[i] = (own32[i] + drecv[i].astype(F32)).astype(BF16)
        g_copy(i).start()
        return carry

    d_copy(0).wait_recv()
    result = own32[0] + drecv[0].astype(F32)
    lax.fori_loop(1, 4, send_out, 0)
    for b in range(1, 4):
        d_copy(b).wait_recv()
        lax.fori_loop(4 * b, 4 * b + 4, send_out, 0)

    for slot, (kind, c) in enumerate(slots):
        for d in (RIGHT, LEFT):
            def a_sent(s, carry, d=d, slot=slot, kind=kind, c=c):
                a_copy(d, s, slot, column(kind), z, c).wait_send()
                return carry

            lax.fori_loop(0, 8 if carried(d, slot, True) else 7, a_sent, 0)
    for c in range(NCH):
        ay_copy(y, z, c).wait_send()

    def sent(i, carry):
        zz = zmod(z + i)
        for c in range(NOTHER, NCH):
            ay_copy(y, zz, c).wait_send()
        return carry

    lax.fori_loop(1, NZ, sent, 0)

    def sent_each(i, carry):
        for c in range(2):
            cy_copy(i, y, c).wait_send()
        ey_copy(i, 1 - y).wait_send()
        return carry

    lax.fori_loop(0, NZ, sent_each, 0)
    for c in range(2):
        for d in (RIGHT, LEFT):
            def c_sent(s, carry, d=d, c=c):
                c_copy(d, s, c, z).wait_send()
                return carry

            def e_sent(s, carry, d=d, c=c):
                e_copy(d, s, c).wait_send()
                return carry

            lax.fori_loop(0, 8 if c == d else 7, c_sent, 0)
            lax.fori_loop(0 if c == d else 1, 8, e_sent, 0)
    for b in range(4):
        d_copy(b).wait_send()

    def g_sent(i, carry):
        g_copy(i).wait_send()
        return carry

    lax.fori_loop(1, NCHIP, g_sent, 0)

    def gather_sum(i, result):
        g_copy(i).wait_recv()
        return result + grecv[i].astype(F32)

    gw_out[...] = lax.fori_loop(1, NCHIP, gather_sum, result)


def per_device(prompt_hidden, kv_weight, queries, resp_keys, resp_values, upstream, signs, lengths):
    vmem = pl.BlockSpec(memory_space=pltpu.VMEM)
    anywhere = pl.BlockSpec(memory_space=pl.ANY)
    dma = pltpu.SemaphoreType.DMA
    nslot = NCH + NOTHER
    grad_keys, grad_values, grad_weight = pl.pallas_call(
        kernel,
        out_shape=(
            jax.ShapeDtypeStruct((SEQ, 1024), BF16),
            jax.ShapeDtypeStruct((SEQ, 1024), BF16),
            jax.ShapeDtypeStruct((64, 128), F32),
        ),
        in_specs=[anywhere] * 6 + [vmem] * 2,
        out_specs=(vmem, vmem, vmem),
        scratch_shapes=[
            pltpu.VMEM((2, NZ, 8, D), BF16),
            pltpu.VMEM((PROMPT, D), BF16),
            pltpu.VMEM((64, D), BF16),
            pltpu.VMEM((SEQ, D), BF16),
            pltpu.VMEM((SEQ, 1024), BF16),
            pltpu.VMEM((SEQ, 1024), BF16),
            pltpu.VMEM((SEQ, D), BF16),
            pltpu.VMEM((KV_HEADS, HEAD, 512), BF16),
            pltpu.VMEM((KV_HEADS, HEAD, 512), BF16),
            pltpu.VMEM((KV_HEADS, HEAD, SEQ), BF16),
            pltpu.VMEM((KV_HEADS, HEAD, SEQ), BF16),
            pltpu.VMEM((NZ, 2, 64, PROMPT), BF16),
            pltpu.VMEM((512, PROMPT + SEQ), BF16),
            pltpu.VMEM((512, PROMPT + SEQ), BF16),
            pltpu.VMEM((NZ, 2, 64, PROMPT), BF16),
            pltpu.VMEM((NZ, 64, PROMPT), BF16),
            pltpu.VMEM((2, 8, 64, PROMPT), BF16),
            pltpu.VMEM((2, 8, 64, PROMPT), BF16),
            pltpu.VMEM((NCHIP, 64, 128), F32),
            pltpu.VMEM((NCHIP, 64, 128), BF16),
            pltpu.VMEM((NCHIP, 64, 128), BF16),
            pltpu.VMEM((NCHIP, 64, 128), BF16),
            pltpu.VMEM((NCHIP, 64, 128), BF16),
            dma((6,)),
            dma((2, 8, nslot)), dma((2, 8, nslot)), dma((NZ, NCH)), dma((NZ, NCH)),
            dma((2, 8, 2)), dma((2, 8, 2)), dma((NZ, 2)), dma((NZ, 2)),
            dma((2, 8, 2)), dma((2, 8, 2)), dma((NZ,)), dma((NZ,)),
            dma((4,)), dma((4,)), dma((NCHIP,)), dma((NCHIP,)),
        ],
        compiler_params=pltpu.CompilerParams(
            collective_id=0, has_side_effects=True, vmem_limit_bytes=63 * 1024 * 1024
        ),
    )(
        prompt_hidden[0], kv_weight, queries[0], resp_keys[0], resp_values[0], upstream[0],
        signs, lengths,
    )
    return grad_keys[None], grad_values[None], grad_weight


def solution(mesh):
    rows = P("group", "resp", None)
    return jax.shard_map(
        per_device,
        mesh=mesh,
        in_specs=(rows, P("resp", None), rows, rows, rows, rows, P("group", "resp"), P("group", "resp")),
        out_specs=(rows, rows, P("resp", "group")),
        check_vma=False,
    )
```

time: 421 us -> 138 us (0.33)
  waiting for transfers between devices: 265 us -> 0 us
  Pallas kernels: 0 us -> 133 us
  matrix products: 84.4 us -> 0 us
  blocking collectives: 22.6 us -> 0 us
  local copies, waits for them, and re-layouts: 16.9 us -> 3.09 us
  between operations: 14.6 us -> 1.3 us
  starting transfers between devices: 7.61 us -> 0 us
  other arithmetic: 6.95 us -> 0 us
    all_gather x2 -> x0, waiting for transfers between devices: 138 us -> none  [gathered_by_axis(): value = lax.all_gather(value, axis, axis=dim, tiled=True)]
    pallas_call x0 -> x1, Pallas kernels: none -> 133 us  [per_device(): pl.pallas_call(kernel, out_shape=(jax.ShapeDtypeStruct((SEQ, 1024), BF16)...]
    reduce_scatter x2 -> x0, waiting for transfers between devices: 99.5 us -> none  [summed_rows(): value = lax.psum_scatter(value, axis, scatter_dimension=dim, tiled=True)]
    dot_general x66 -> x0, matrix products: 84.4 us -> none  [the longest x8 15.8 us: attend_group(): jnp.einsum('qrp,rqd->dp', prompt_sgrad, queries, preferred_element_type=j...]
    all_to_all x1 -> x0, waiting for transfers between devices: 27.9 us -> none  [sent_and_summed(): lax.all_to_all(blocks, axis, split_axis=0, concat_axis=0, tiled=True)]
    all_gather x2 -> x0, blocking collectives: 22.6 us -> none  [gathered_by_axis(): value = lax.all_gather(value, axis, axis=dim, tiled=True)]
    dynamic_slice x16 -> x0, local copies, waits for them, and re-layouts: 8.42 us -> none  [per_device(): lax.map(attend_group, (query_heads, cotangent_heads, own_keys, own_values...]
    all_to_all x1 -> x0, starting transfers between devices: 7.45 us -> none  [sent_and_summed(): lax.all_to_all(blocks, axis, split_axis=0, concat_axis=0, tiled=True)]
  transfers between devices with their start and end apart: 5 -> 0, of which waited for: 5 -> 0; matrix products, arithmetic and copies ran while one was open for 2% -> 0% of each run, Pallas kernels for 0% -> 0%
where the time goes in v1:
time: 138 us
  Pallas kernels  133 us (96%)
  local copies, waits for them, and re-layouts  3.09 us (2%)
    pallas_call x1, Pallas kernels, per_device(): pl.pallas_call(kernel, out_shape=(jax.ShapeDtypeStruct((SEQ, 1024), BF16)...  133 us
    unnamed x7, local copies, waits for them, and re-layouts  3.09 us

profile of v1, /device:TPU:8, one launch (start us, length us, event | category | flops | bytes accessed | tf_op | source)
XLA Modules:
  0.0 137.8 jit_solution(9881544975334365283)
XLA Ops:
  1.3 133.4 %shard_map.103 = (bf16[128,1024]{1,0:T(8,128)(2,1)}, bf16[128,1024]{1,0:T(8,128)(2,1)}, f32[64,128]{1,0:T(8,128)}) custom-call(bf16[8,4096]{1,0:T(8,128)(2,1)} %bitcast.13, bf16[64,4096]{1,0:T(8,128)(2,1)} %w_in.1, bf16[128,4096]{1,0:T(8,128)(2,1)} %bitcast.7, bf16[128,1024]{1,0:T(8,128)(2,1)} %bitcast.9, bf16[128,1024]{1,0:T(8,128)(2,1)} %bitcast.10, ...), custom_call_target="tpu_custom_call" | custom-call | tf_op jit(solution)/shard_map/pallas_call | solution.py:428
  134.7 0.0 copy-start
  134.7 1.7 %copy.15 = bf16[1,128,1024]{2,1,0:T(8,128)(2,1)} copy(bf16[1,128,1024]{2,1,0:T(8,128)(2,1)} %bitcast.12) | data formatting | bytes 524288
  136.4 0.0 copy-done
  136.4 0.0 copy-start.1
  136.5 0.7 copy.16
  137.2 0.1 copy-done.1
  137.2 0.6 copy.17
Async XLA Ops:
  134.7 1.7 %copy-start = (bf16[128,1024]{1,0:T(8,128)(2,1)S(1)}, bf16[128,1024]{1,0:T(8,128)(2,1)}, u32[]{:S(2)}) copy-start(bf16[128,1024]{1,0:T(8,128)(2,1)} %get-tuple-element.7) | copy-start | bytes 786436
  136.4 0.8 copy-start.1

commit v2 on v1

--- a/solution.py
+++ b/solution.py
@@ -19,10 +19,24 @@
 PROMPT = 256
 NZ = 16
 NCHIP = 16
-NCH = 4
-NOTHER = 2
+NCH = 2
+NOTHER = 0
 CW = D // NCH
-RIGHT, LEFT = 0, 1
+CHILDREN = {
+    0: (4, -4, 1, -1), 4: (8, 6, 5, 3), -4: (8, -6, -5, -3),
+    1: (2,), -1: (-2,), 6: (7,), -6: (-7,),
+}
+ARRIVALS = ((4, -4), (1, -1), (6, -6), (2, -2), (5, -5), (3, -3), (8,), (7, -7))
+A_CHILDREN = {0: (2, -2, 1, -1), 2: (4, 3), -2: (-4, -3), 4: (6, 5), -4: (-6, -5), 6: (8, 7), -6: (8, -7)}
+A_ARRIVALS = ((2, -2), (1, -1), (4, -4), (3, -3), (6, -6), (5, -5), (8,), (7, -7))
+A_SENDS = tuple((o, child) for o, children in A_CHILDREN.items() for child in children)
+MOVES = (1, -1, 2, -2, 4, -4)
+SENDS = tuple((o, child) for o, children in CHILDREN.items() for child in children)
+HEAD_ORDER = sum(k * 8**i for i, k in enumerate((4, 0, 1, 7, 5, 3, 2, 6)))
+
+
+def takes(o, child, index, count):
+    return child != 8 or (o > 0) == (index < (count + 1) // 2)
 
 
 def kernel(
@@ -41,12 +55,11 @@
     def zmod(value):
         return lax.rem(value + 2 * NZ, NZ)
 
-    up_z = {"resp": zmod(z + 1) * 2 + y}
-    down_z = {"resp": zmod(z - 1) * 2 + y}
     partner = {"resp": z * 2 + 1 - y}
     twin = {"group": chip * 2 + 1 - core}
-    to = (up_z, down_z)
-    sign = (-1, 1)
+
+    def along(step):
+        return {"resp": zmod(z + step) * 2 + y}
 
     def peer(i):
         return lax.rem(chip + i, NCHIP)
@@ -63,7 +76,7 @@
         load.start()
 
     barrier = pltpu.get_barrier_semaphore()
-    for target in (up_z, down_z, partner, twin):
+    for target in (partner, twin, *map(along, MOVES)):
         pl.semaphore_signal(barrier, inc=1, device_id=target, device_id_type=MESH)
 
     def greet(i, carry):
@@ -73,18 +86,29 @@
         return carry
 
     lax.fori_loop(1, NCHIP, greet, 0)
-    pl.semaphore_wait(barrier, NCHIP - 1 + 4)
+    pl.semaphore_wait(barrier, NCHIP - 1 + 2 + len(MOVES))
     loads[0].wait()
 
     def hid_piece(col, zz, c):
         return hid.at[col, zz, :, pl.ds(c * CW, CW)]
 
-    def a_copy(d, s, slot, col, zz, c):
-        return pltpu.make_async_remote_copy(
-            src_ref=hid_piece(col, zz, c), dst_ref=hid_piece(col, zz, c),
-            send_sem=a_send.at[d, s, slot], recv_sem=a_recv.at[d, s, slot],
-            device_id=to[d], device_id_type=MESH,
-        )
+    def a_copy(o, child, slot):
+        kind, c = slots[slot]
+        piece = hid_piece(column(kind), zmod(z - o), c)
+        return pltpu.make_async_remote_copy(
+            src_ref=piece, dst_ref=piece,
+            send_sem=a_send.at[child % NZ, slot], recv_sem=a_recv.at[child % NZ, slot],
+            device_id=along(child - o), device_id_type=MESH,
+        )
+
+    def a_arrived(o, slot):
+        kind, c = slots[slot]
+        piece = hid_piece(column(kind), zmod(z - o), c)
+        pltpu.make_async_remote_copy(
+            src_ref=piece, dst_ref=piece,
+            send_sem=a_send.at[o % NZ, slot], recv_sem=a_recv.at[o % NZ, slot],
+            device_id=partner, device_id_type=MESH,
+        ).wait_recv()
 
     def ay_copy(col, zz, c):
         return pltpu.make_async_remote_copy(
@@ -98,30 +122,23 @@
     def column(kind):
         return y if kind == 0 else 1 - y
 
-    def carried(d, slot, s_last):
+    def a_takes(o, child, slot):
         kind, c = slots[slot]
-        if not s_last:
-            return True
-        half = (NCH if kind == 0 else NOTHER) // 2
-        return (c < half) == (d == RIGHT)
-
-    for c in range(NCH):
-        ay_copy(y, z, c).start()
-    for slot, (kind, c) in enumerate(slots):
-        for d in (RIGHT, LEFT):
-            if kind == 1 and d == RIGHT:
-                ay_copy(1 - y, z, c).wait_recv()
-            a_copy(d, 0, slot, column(kind), z, c).start()
-
-    def a_step(s, last):
-        for slot, (kind, c) in enumerate(slots):
-            for d in (RIGHT, LEFT):
-                zz = zmod(z + sign[d] * s)
-                a_copy(d, s - 1, slot, column(kind), zz, c).wait_recv()
-                if carried(d, slot, last):
-                    a_copy(d, s, slot, column(kind), zz, c).start()
-                if kind == 0 and c >= NOTHER:
-                    ay_copy(y, zz, c).start()
+        return takes(o, child, c, NCH if kind == 0 else NOTHER)
+
+    def a_forward(o, slot, children):
+        for child in children:
+            if a_takes(o, child, slot):
+                a_copy(o, child, slot).start()
+
+    for at, children in enumerate((A_CHILDREN[0][:2], A_CHILDREN[0][2:])):
+        for slot in range(NCH):
+            a_forward(0, slot, children)
+            if at == 0:
+                ay_copy(y, z, slot).start()
+    for slot in range(NCH, NCH + NOTHER):
+        ay_copy(1 - y, z, slots[slot][1]).wait_recv()
+        a_forward(0, slot, A_CHILDREN[0])
 
     def prepare(j):
         weights = jnp.where(
@@ -140,22 +157,19 @@
 
     for load in loads[1:]:
         load.wait()
-    prepare(0)
-
-    def a_loop(s, carry):
-        a_step(s, False)
-        prepare(s)
-        return carry
-
-    lax.fori_loop(1, 7, a_loop, 0)
-    a_step(7, True)
-    prepare(7)
-    far = zmod(z + 8)
-    for slot, (kind, c) in enumerate(slots):
-        d = RIGHT if carried(RIGHT, slot, True) else LEFT
-        a_copy(d, 7, slot, column(kind), far, c).wait_recv()
-        if kind == 0 and c >= NOTHER:
-            ay_copy(y, far, c).start()
+
+    def prepare_loop(j, carry):
+        prepare(j)
+        return carry
+
+    lax.fori_loop(0, KV_HEADS, prepare_loop, 0)
+    for offsets in A_ARRIVALS:
+        for slot, (kind, c) in enumerate(slots):
+            for o in offsets:
+                a_arrived(o, slot)
+                a_forward(o, slot, A_CHILDREN.get(o, ()))
+                if kind == 0 and c >= NOTHER:
+                    ay_copy(y, zmod(z - o), c).start()
     for c in range(NOTHER, NCH):
         ay_copy(1 - y, z, c).wait_recv()
 
@@ -183,12 +197,26 @@
     def kv_piece(zz, col, c):
         return kvb.at[zz, col, pl.ds(c * 32, 32), :]
 
-    def c_copy(d, s, c, zz):
-        return pltpu.make_async_remote_copy(
-            src_ref=kv_piece(zz, y, c), dst_ref=kv_piece(zz, y, c),
-            send_sem=c_send.at[d, s, c], recv_sem=c_recv.at[d, s, c],
-            device_id=to[d], device_id_type=MESH,
-        )
+    def c_copy(o, child, c):
+        piece = kv_piece(zmod(z - o), y, c)
+        return pltpu.make_async_remote_copy(
+            src_ref=piece, dst_ref=piece,
+            send_sem=c_send.at[child % NZ, c], recv_sem=c_recv.at[child % NZ, c],
+            device_id=along(child - o), device_id_type=MESH,
+        )
+
+    def c_arrived(o, c):
+        piece = kv_piece(zmod(z - o), y, c)
+        pltpu.make_async_remote_copy(
+            src_ref=piece, dst_ref=piece,
+            send_sem=c_send.at[o % NZ, c], recv_sem=c_recv.at[o % NZ, c],
+            device_id=partner, device_id_type=MESH,
+        ).wait_recv()
+
+    def c_forward(o, c, children):
+        for child in children:
+            if takes(o, child, c, 2):
+                c_copy(o, child, c).start()
 
     def cy_copy(zz, col, c):
         return pltpu.make_async_remote_copy(
@@ -197,41 +225,33 @@
             device_id=partner, device_id_type=MESH,
         )
 
-    for c in range(2):
-        for d in (RIGHT, LEFT):
-            c_copy(d, 0, c, z).start()
-        cy_copy(z, y, c).start()
-
-    def c_step(s, last):
-        for c in range(2):
-            for d in (RIGHT, LEFT):
-                zz = zmod(z + sign[d] * s)
-                c_copy(d, s - 1, c, zz).wait_recv()
-                if not last or c == d:
-                    c_copy(d, s, c, zz).start()
-                cy_copy(zz, y, c).start()
-
-    def c_loop(s, carry):
-        c_step(s, False)
-        return carry
-
-    lax.fori_loop(1, 7, c_loop, 0)
-    c_step(7, True)
-    for c in range(2):
-        c_copy(c, 7, c, far).wait_recv()
-        cy_copy(far, y, c).start()
-
-    def cy_wait(i, carry):
-        for c in range(2):
-            cy_copy(zmod(z + i), 1 - y, c).wait_recv()
-        return carry
-
-    lax.fori_loop(0, NZ, cy_wait, 0)
+    for children in ((4, -4), (1, -1)):
+        for c in range(2):
+            c_forward(0, c, children)
+            if children[0] == 4:
+                cy_copy(z, y, c).start()
+    for offsets in ARRIVALS:
+        for c in range(2):
+            for o in offsets:
+                c_arrived(o, c)
+                c_forward(o, c, CHILDREN.get(o, ()))
+                cy_copy(zmod(z - o), y, c).start()
 
     scaling = 1.0 / math.sqrt(HEAD)
     factor = scaling * math.log2(math.e)
 
-    def attend(j, carry):
+    def ey_copy(zz, col):
+        return pltpu.make_async_remote_copy(
+            src_ref=terms.at[zz, col], dst_ref=yrecv.at[zz],
+            send_sem=ey_send.at[zz], recv_sem=ey_recv.at[zz],
+            device_id=partner, device_id_type=MESH,
+        )
+
+    def attend(step, order):
+        j = lax.rem(z + order % 8, 8)
+        for c in range(2):
+            cy_copy(j, 1 - y, c).wait_recv()
+            cy_copy(j + 8, 1 - y, c).wait_recv()
         keys = jnp.concatenate([kvb[j].reshape(HEAD, PROMPT), kt_own[j]], axis=1)
         values = jnp.concatenate([kvb[j + 8].reshape(HEAD, PROMPT), vt_own[j]], axis=1)
         shape = (SEQ, PROMPT + SEQ)
@@ -255,77 +275,47 @@
         value_grad = jnp.dot(ct[j], ph[...], preferred_element_type=F32)
         terms[j] = key_grad[:, :PROMPT].astype(BF16).reshape(2, 64, PROMPT)
         terms[j + 8] = value_grad[:, :PROMPT].astype(BF16).reshape(2, 64, PROMPT)
+        ey_copy(j, 1 - y).start()
+        ey_copy(j + 8, 1 - y).start()
         cols = pl.ds(pl.multiple_of(j * HEAD, HEAD), HEAD)
         gk_out[:, cols] = key_grad[:, PROMPT:].T.astype(BF16)
         gv_out[:, cols] = value_grad[:, PROMPT:].T.astype(BF16)
-        return carry
-
-    lax.fori_loop(0, KV_HEADS, attend, 0)
-
-    def ey_copy(zz, col):
-        return pltpu.make_async_remote_copy(
-            src_ref=terms.at[zz, col], dst_ref=yrecv.at[zz],
-            send_sem=ey_send.at[zz], recv_sem=ey_recv.at[zz],
-            device_id=partner, device_id_type=MESH,
-        )
-
-    def e_copy(d, s, c):
+        return order // 8
+
+    lax.fori_loop(0, KV_HEADS, attend, HEAD_ORDER)
+
+    def e_copy(o, parent):
+        part = pl.ds(0, 64) if o != 8 else pl.ds(0 if parent == 4 else 32, 32)
+        return pltpu.make_async_remote_copy(
+            src_ref=esend.at[o % NZ, part, :], dst_ref=erecv.at[o % NZ, part, :],
+            send_sem=e_send.at[o % NZ, int(parent < 0)],
+            recv_sem=e_recv.at[o % NZ, int(parent < 0)],
+            device_id=along(parent - o), device_id_type=MESH,
+        )
+
+    def partial(o, c):
+        zz = zmod(z - o)
         part = pl.ds(c * 32, 32)
-        return pltpu.make_async_remote_copy(
-            src_ref=esend.at[d, s, part, :], dst_ref=erecv.at[d, s, part, :],
-            send_sem=e_send.at[d, s, c], recv_sem=e_recv.at[d, s, c],
-            device_id=to[d], device_id_type=MESH,
-        )
-
-    ey_copy(far, 1 - y).start()
-
-    def ey_start(i, carry):
-        ey_copy(zmod(z + 8 - i), 1 - y).start()
-        ey_copy(zmod(z + 8 + i), 1 - y).start()
-        return carry
-
-    lax.fori_loop(1, 8, ey_start, 0)
-    ey_copy(z, 1 - y).start()
-
-    def pair_sum(zz, c):
-        part = pl.ds(c * 32, 32)
-        return terms[zz, y, part, :].astype(F32) + yrecv[zz, part, :].astype(F32)
-
-    ey_copy(far, y).wait_recv()
-    for d in (RIGHT, LEFT):
-        esend[d, 0, pl.ds(d * 32, 32), :] = pair_sum(far, d).astype(BF16)
-        e_copy(d, 0, d).start()
-
-    def e_step(s, first):
-        for d in (RIGHT, LEFT):
-            ey_copy(zmod(z + sign[d] * (s - 8)), y).wait_recv()
-        for c in range(2):
-            part = pl.ds(c * 32, 32)
-            for d in (RIGHT, LEFT):
-                value = pair_sum(zmod(z + sign[d] * (s - 8)), c)
-                if not first or c == d:
-                    e_copy(d, s - 1, c).wait_recv()
-                    value = value + erecv[d, s - 1, part, :].astype(F32)
-                esend[d, s, part, :] = value.astype(BF16)
-                e_copy(d, s, c).start()
-
-    e_step(1, True)
-
-    def e_loop(s, carry):
-        e_step(s, False)
-        return carry
-
-    lax.fori_loop(2, 8, e_loop, 0)
-    ey_copy(z, y).wait_recv()
-    halves = []
-    for c in range(2):
-        part = pl.ds(c * 32, 32)
-        value = pair_sum(z, c)
-        for d in (RIGHT, LEFT):
-            e_copy(d, 7, c).wait_recv()
-            value = value + erecv[d, 7, part, :].astype(F32)
-        halves.append(value.astype(BF16))
-    prompt_grad = jnp.concatenate(halves, axis=0)
+        value = terms[zz, y, part, :].astype(F32) + yrecv[zz, part, :].astype(F32)
+        for child in CHILDREN.get(o, ()):
+            if child != 8 or (o > 0) == (c == 0):
+                value = value + erecv[child % NZ, part, :].astype(F32)
+        return value.astype(BF16)
+
+    def collect(o):
+        ey_copy(zmod(z - o), y).wait_recv()
+        for child in CHILDREN.get(o, ()):
+            e_copy(child, o).wait_recv()
+
+    for o in (7, -7, 8, 5, -5, 3, -3, 2, -2, 6, -6, 1, -1, 4, -4):
+        collect(o)
+        for c in range(2):
+            esend[o % NZ, pl.ds(c * 32, 32), :] = partial(o, c)
+        for parent, children in CHILDREN.items():
+            if o in children:
+                e_copy(o, parent).start()
+    collect(0)
+    prompt_grad = jnp.concatenate([partial(0, c) for c in range(2)], axis=0)
 
     def d_copy(b):
         part = pl.ds(b * 4, 4)
@@ -367,13 +357,10 @@
         d_copy(b).wait_recv()
         lax.fori_loop(4 * b, 4 * b + 4, send_out, 0)
 
-    for slot, (kind, c) in enumerate(slots):
-        for d in (RIGHT, LEFT):
-            def a_sent(s, carry, d=d, slot=slot, kind=kind, c=c):
-                a_copy(d, s, slot, column(kind), z, c).wait_send()
-                return carry
-
-            lax.fori_loop(0, 8 if carried(d, slot, True) else 7, a_sent, 0)
+    for o, child in A_SENDS:
+        for slot in range(len(slots)):
+            if a_takes(o, child, slot):
+                a_copy(o, child, slot).wait_send()
     for c in range(NCH):
         ay_copy(y, z, c).wait_send()
 
@@ -392,18 +379,11 @@
         return carry
 
     lax.fori_loop(0, NZ, sent_each, 0)
-    for c in range(2):
-        for d in (RIGHT, LEFT):
-            def c_sent(s, carry, d=d, c=c):
-                c_copy(d, s, c, z).wait_send()
-                return carry
-
-            def e_sent(s, carry, d=d, c=c):
-                e_copy(d, s, c).wait_send()
-                return carry
-
-            lax.fori_loop(0, 8 if c == d else 7, c_sent, 0)
-            lax.fori_loop(0 if c == d else 1, 8, e_sent, 0)
+    for o, child in SENDS:
+        for c in range(2):
+            if takes(o, child, c, 2):
+                c_copy(o, child, c).wait_send()
+        e_copy(child, o).wait_send()
     for b in range(4):
         d_copy(b).wait_send()
 
@@ -451,17 +431,17 @@
             pltpu.VMEM((512, PROMPT + SEQ), BF16),
             pltpu.VMEM((NZ, 2, 64, PROMPT), BF16),
             pltpu.VMEM((NZ, 64, PROMPT), BF16),
-            pltpu.VMEM((2, 8, 64, PROMPT), BF16),
-            pltpu.VMEM((2, 8, 64, PROMPT), BF16),
+            pltpu.VMEM((NZ, 64, PROMPT), BF16),
+            pltpu.VMEM((NZ, 64, PROMPT), BF16),
             pltpu.VMEM((NCHIP, 64, 128), F32),
             pltpu.VMEM((NCHIP, 64, 128), BF16),
             pltpu.VMEM((NCHIP, 64, 128), BF16),
             pltpu.VMEM((NCHIP, 64, 128), BF16),
             pltpu.VMEM((NCHIP, 64, 128), BF16),
             dma((6,)),
-            dma((2, 8, nslot)), dma((2, 8, nslot)), dma((NZ, NCH)), dma((NZ, NCH)),
-            dma((2, 8, 2)), dma((2, 8, 2)), dma((NZ, 2)), dma((NZ, 2)),
-            dma((2, 8, 2)), dma((2, 8, 2)), dma((NZ,)), dma((NZ,)),
+            dma((NZ, nslot)), dma((NZ, nslot)), dma((NZ, NCH)), dma((NZ, NCH)),
+            dma((NZ, 2)), dma((NZ, 2)), dma((NZ, 2)), dma((NZ, 2)),
+            dma((NZ, 2)), dma((NZ, 2)), dma((NZ,)), dma((NZ,)),
             dma((4,)), dma((4,)), dma((NCHIP,)), dma((NCHIP,)),
         ],
         compiler_params=pltpu.CompilerParams(

time: 138 us -> 110 us (0.80)
  Pallas kernels: 133 us -> 106 us
    pallas_call x1, Pallas kernels: 133 us -> 106 us  [per_device(): pl.pallas_call(kernel, out_shape=(jax.ShapeDtypeStruct((SEQ, 1024), BF16)...]
where the time goes in v2:
time: 110 us
  Pallas kernels  106 us (96%)
  local copies, waits for them, and re-layouts  3.09 us (3%)
  between operations  1.3 us (1%)
    pallas_call x1, Pallas kernels, per_device(): pl.pallas_call(kernel, out_shape=(jax.ShapeDtypeStruct((SEQ, 1024), BF16)...  106 us
    unnamed x7, local copies, waits for them, and re-layouts  3.09 us

profile of v2, /device:TPU:8, one launch (start us, length us, event | category | flops | bytes accessed | tf_op | source)
XLA Modules:
  0.0 110.1 jit_solution(7028394167366907118)
XLA Ops:
  1.3 105.7 %shard_map.103 = (bf16[128,1024]{1,0:T(8,128)(2,1)}, bf16[128,1024]{1,0:T(8,128)(2,1)}, f32[64,128]{1,0:T(8,128)}) custom-call(bf16[8,4096]{1,0:T(8,128)(2,1)} %bitcast.13, bf16[64,4096]{1,0:T(8,128)(2,1)} %w_in.1, bf16[128,4096]{1,0:T(8,128)(2,1)} %bitcast.7, bf16[128,1024]{1,0:T(8,128)(2,1)} %bitcast.9, bf16[128,1024]{1,0:T(8,128)(2,1)} %bitcast.10, ...), custom_call_target="tpu_custom_call" | custom-call | tf_op jit(solution)/shard_map/pallas_call | solution.py:408
  107.0 0.0 copy-start
  107.0 1.7 %copy.15 = bf16[1,128,1024]{2,1,0:T(8,128)(2,1)} copy(bf16[1,128,1024]{2,1,0:T(8,128)(2,1)} %bitcast.12) | data formatting | bytes 524288
  108.7 0.0 copy-done
  108.7 0.0 copy-start.1
  108.7 0.7 copy.16
  109.4 0.1 copy-done.1
  109.4 0.6 copy.17
Async XLA Ops:
  107.0 1.7 %copy-start = (bf16[128,1024]{1,0:T(8,128)(2,1)S(1)}, bf16[128,1024]{1,0:T(8,128)(2,1)}, u32[]{:S(2)}) copy-start(bf16[128,1024]{1,0:T(8,128)(2,1)} %get-tuple-element.7) | copy-start | bytes 786436
  108.7 0.8 copy-start.1
